TPU v7x, 256 devices: a whole 4x4x8 slice. The times are simulated.
256 devices in a mesh: ctx: 32 (over y, z), head: 8 (over x, core).
Axes of the slice: x: 4, y: 4, z: 8, core: 2. Of those that a mesh axis runs over, the one named last changes fastest.
Arguments:
- q_first: bfloat16 [768, 4096], P('head'), may hold values from -24 to 24
- q_second: bfloat16 [768, 4096], P('head'), may hold values from -24 to 24
- k_cache: bfloat16 [131072, 16, 128], P('ctx', 'head'), may hold values from -8 to 8
- v_cache: bfloat16 [131072, 16, 128], P('ctx', 'head'), may hold values from -6 to 6
- kept_blocks: int32 [32, 32], P('ctx'), may hold values from 0 to 31, as said below
- kept_count: int32 [32], P('ctx'), may hold values from 1 to 32, 256 in all
Outputs:
- out_first: bfloat16 [768, 4096], P('ctx', 'head')
- out_second: bfloat16 [768, 4096], P('ctx', 'head')
Inputs may be any that keep to these rules, and one draw needn't show every extreme that they name: `kept_blocks`: row s lists distinct block numbers of shard s; only its first kept_count[s] entries are kept. `kept_count`: the counts sum to 256; the largest is 32.
All inputs are finite; a program needn't handle non-finite values. No bound on the sum of `kept_count` on one device may be relied on, other than what follows from the above.
Results may differ from a plain program's by a relative error of at most 0.022.
Values may be sent and summed in bfloat16 or wider, within the bound.
A program may use at most 64 MiB of HBM per device.

v0:
```python
import math

import jax
import jax.numpy as jnp
from jax import lax
from jax.sharding import PartitionSpec as P

HD = 128
QPS = 168
BLK = 128


def in_one_piece(arrays, axis, split_dim, concat_dim, along):
    ends, at = ([], 0)
    for a in arrays[:-1]:
        at += a.shape[along]
        ends.append(at)
    both = jnp.concatenate(arrays, axis=along)
    return tuple(
        jnp.split(
            lax.all_to_all(both, axis, split_axis=split_dim, concat_axis=concat_dim, tiled=True),
            ends,
            axis=along,
        )
    )


def absorb(running, head_queries, key_part, value_part, usable):
    row_top, row_total, summed = running
    scores = jnp.einsum(
        "gqd,kgd->gqk", head_queries, key_part, preferred_element_type=jnp.float32
    ) * QPS ** (-0.5)
    if usable is not None:
        scores = jnp.where(usable[None, None, :], scores, -jnp.inf)
    newtop = jnp.maximum(row_top, jnp.max(scores, axis=2))
    factor = jnp.exp(row_top - newtop)
    weights = jnp.exp(scores - newtop[:, :, None])
    row_total = row_total * factor + jnp.sum(weights, axis=2)
    summed = summed * factor[:, :, None] + jnp.einsum(
        "gqk,kgd->gqd", weights.astype(jnp.bfloat16), value_part, preferred_element_type=jnp.float32
    )
    return (newtop, row_total, summed)


def start_carry(head_queries):
    kv_local, row_count, head_width = head_queries.shape
    return (
        jnp.full((kv_local, row_count), -1e30, jnp.float32),
        jnp.zeros((kv_local, row_count), jnp.float32),
        jnp.zeros((kv_local, row_count, head_width), jnp.float32),
    )


def sweep_keys(running, head_queries, keys, values):
    length = keys.shape[0]
    block_keys = math.gcd(length, 512)

    def absorb_block(step_index, current):
        key_part = lax.dynamic_slice_in_dim(keys, step_index * block_keys, block_keys, 0)
        value_part = lax.dynamic_slice_in_dim(values, step_index * block_keys, block_keys, 0)
        return absorb(current, head_queries, key_part, value_part, None)

    return lax.fori_loop(0, length // block_keys, absorb_block, running)


def to_rows(running, row_count, group_size):
    row_top, row_total, summed = running
    kv_local = row_top.shape[0]
    head_count = kv_local * group_size
    row_top = (
        row_top.reshape(kv_local, row_count, group_size)
        .transpose(1, 0, 2)
        .reshape(row_count, head_count)
    )
    row_total = (
        row_total.reshape(kv_local, row_count, group_size)
        .transpose(1, 0, 2)
        .reshape(row_count, head_count)
    )
    summed = (
        summed.reshape(kv_local, row_count, group_size, HD)
        .transpose(1, 0, 2, 3)
        .reshape(row_count, head_count * HD)
    )
    return (row_top, row_total, summed)


def combine(row_top, row_total, summed):
    head_count = row_top.shape[1]
    all_tops, totals, all_sums = in_one_piece(
        (row_top[None], row_total[None], summed[None]), "ctx", 1, 0, 2
    )
    best_top = jnp.max(all_tops, axis=0)
    factor = jnp.exp(all_tops - best_top[None])
    owned = all_sums.shape[1]
    numerator = jnp.sum(
        all_sums.reshape(-1, owned, head_count, HD) * factor[:, :, :, None], axis=0
    ).reshape(owned, head_count * HD)
    denominator = jnp.sum(totals * factor, axis=0)
    owned = numerator.shape[0]
    result = numerator.reshape(owned, head_count, HD) / denominator[:, :, None]
    return result.reshape(owned, head_count * HD).astype(jnp.bfloat16)


def shards(q_first, q_second, k_cache, v_cache, kept_blocks, kept_count):
    local_first, local_second = (
        lax.all_to_all(q_first, "head", split_axis=1, concat_axis=0, tiled=True),
        lax.all_to_all(q_second, "head", split_axis=1, concat_axis=0, tiled=True),
    )
    kv_local = k_cache.shape[1]
    row_count = local_first.shape[0]
    group_size = local_first.shape[1] // (kv_local * HD)

    def by_head(query_block):
        return (
            query_block.reshape(row_count, kv_local, group_size, HD)
            .transpose(1, 0, 2, 3)
            .reshape(kv_local, row_count * group_size, HD)
        )

    heads_first = by_head(local_first)
    heads_second = by_head(local_second)
    blocks_here = k_cache.shape[0] // BLK
    key_blocks = k_cache.reshape(blocks_here, BLK, kv_local, HD)
    value_blocks = v_cache.reshape(blocks_here, BLK, kv_local, HD)
    kept_here = kept_count[0]
    chosen = kept_blocks[0]
    state_first = sweep_keys(start_carry(heads_first), heads_first, k_cache, v_cache)
    per_turn = 4
    rounds = (kept_here + per_turn - 1) // per_turn

    def absorb_group(step_index, current):
        slot_ids = step_index * per_turn + jnp.arange(per_turn, dtype=jnp.int32)
        block_ids = lax.dynamic_slice_in_dim(chosen, step_index * per_turn, per_turn, 0)
        key_part = key_blocks[block_ids].reshape(per_turn * BLK, kv_local, HD)
        value_part = value_blocks[block_ids].reshape(per_turn * BLK, kv_local, HD)
        usable = jnp.repeat(slot_ids < kept_here, BLK)
        return absorb(current, heads_second, key_part, value_part, usable)

    state_second = lax.fori_loop(0, rounds, absorb_group, start_carry(heads_second))
    out_first = combine(*to_rows(state_first, row_count, group_size))
    out_second = combine(*to_rows(state_second, row_count, group_size))
    return (out_first, out_second)


def solution(mesh):
    placed = (
        P("head", None),
        P("head", None),
        P("ctx", "head", None),
        P("ctx", "head", None),
        P("ctx", None),
        P("ctx"),
    )
    return jax.shard_map(
        shards,
        mesh=mesh,
        in_specs=placed,
        out_specs=(P("ctx", "head"), P("ctx", "head")),
        check_vma=False,
    )
```

profile of v0, /device:TPU:1, one launch (start us, length us, event | category | flops | bytes accessed | tf_op | source)
XLA Modules:
  0.0 339.6 jit_solution(11179732056554173420)
XLA Ops:
  2.8 6.6 %all-to-all-start.2 = ((bf16[96,8,512]{2,0,1:T(8,128)(2,1)}), bf16[96,8,512]{2,0,1:T(8,128)(2,1)S(1)}, u32[]{:S(2)}, u32[]{:S(2)}) async-start(bf16[96,8,512]{2,0,1:T(8,128)(2,1)} %bitcast.78), calls=%async_computation.2 | async-start | bytes 1572864 | tf_op jit(solution)/shard_map/all_to_all | solution.py:108
  11.1 10.5 %all-to-all-done.2 = bf16[96,8,512]{2,0,1:T(8,128)(2,1)S(1)} async-done(((bf16[96,8,512]{2,0,1:T(8,128)(2,1)}), bf16[96,8,512]{2,0,1:T(8,128)(2,1)S(1)}, u32[]{:S(2)}, u32[]{:S(2)}) %all-to-all-start.2) | async-done | bytes 786464 | tf_op jit(solution)/shard_map/all_to_all | solution.py:108
  21.6 5.1 %all-to-all-start = ((bf16[96,8,512]{2,0,1:T(8,128)(2,1)}), bf16[96,8,512]{2,0,1:T(8,128)(2,1)}, u32[]{:S(2)}, u32[]{:S(2)}) async-start(bf16[96,8,512]{2,0,1:T(8,128)(2,1)} %bitcast.79), calls=%async_computation | async-start | bytes 1572864 | tf_op jit(solution)/shard_map/all_to_all | solution.py:107
  28.7 129.7 %while.32 = (s32[]{:T(128)}, f32[2,1536]{1,0:T(2,128)S(1)}, f32[2,1536]{1,0:T(2,128)S(1)}, f32[2,1536,128]{2,1,0:T(8,128)}, s32[]{:T(128)}, /*index=5*/s32[]{:T(...) while((s32[]{:T(128)}, f32[2,1536]{1,0:T(2,128)S(1)}, ...), condition=%wide.region_10.11_spmd, body=%wide.region_7.10_spmd.sunk | while | flops 823401472 | bytes 49748272 | solution.py:140
  38.6 6.3 %fusion.57 = f32[2,1536,128]{2,1,0:T(8,128)} fusion(f32[2,512,1536]{2,1,0:T(8,128)} %copy-done.1, f32[2,1536]{1,0:T(2,128)S(1)} %max.14, pred[512]{0:T(512)(128)(4,1)S(1)} %broadcast_bitcast_fusion.2, f32[2,1536,128]{2,1,0:T(8,128)} %get-tuple-element.433, f32[2,1536]{1,0:T(2,128)S(1)} %get-tuple-element.402, bf16[512,2,128]{2,1,0:T(2,128)(2,1)S(1)} %bitcast.113), kind=kOutput, calls=%fused_computation.13.clone.1 | convolution fusion | flops 409731072 | bytes 9724416 | tf_op jit(solution)/shard_map/while/body/gqk,kgd->gqd/dot_general | solution.py:39
  54.8 6.3 %fusion.57 = f32[2,1536,128]{2,1,0:T(8,128)} fusion(f32[2,512,1536]{2,1,0:T(8,128)} %copy-done.1, f32[2,1536]{1,0:T(2,128)S(1)} %max.14, pred[512]{0:T(512)(128)(4,1)S(1)} %broadcast_bitcast_fusion.2, f32[2,1536,128]{2,1,0:T(8,128)} %get-tuple-element.433, f32[2,1536]{1,0:T(2,128)S(1)} %get-tuple-element.402, bf16[512,2,128]{2,1,0:T(2,128)(2,1)S(1)} %bitcast.113), kind=kOutput, calls=%fused_computation.13.clone.1 | convolution fusion | flops 409731072 | bytes 9724416 | tf_op jit(solution)/shard_map/while/body/gqk,kgd->gqd/dot_general | solution.py:39
  71.0 6.3 %fusion.57 = f32[2,1536,128]{2,1,0:T(8,128)} fusion(f32[2,512,1536]{2,1,0:T(8,128)} %copy-done.1, f32[2,1536]{1,0:T(2,128)S(1)} %max.14, pred[512]{0:T(512)(128)(4,1)S(1)} %broadcast_bitcast_fusion.2, f32[2,1536,128]{2,1,0:T(8,128)} %get-tuple-element.433, f32[2,1536]{1,0:T(2,128)S(1)} %get-tuple-element.402, bf16[512,2,128]{2,1,0:T(2,128)(2,1)S(1)} %bitcast.113), kind=kOutput, calls=%fused_computation.13.clone.1 | convolution fusion | flops 409731072 | bytes 9724416 | tf_op jit(solution)/shard_map/while/body/gqk,kgd->gqd/dot_general | solution.py:39
  87.3 6.3 %fusion.57 = f32[2,1536,128]{2,1,0:T(8,128)} fusion(f32[2,512,1536]{2,1,0:T(8,128)} %copy-done.1, f32[2,1536]{1,0:T(2,128)S(1)} %max.14, pred[512]{0:T(512)(128)(4,1)S(1)} %broadcast_bitcast_fusion.2, f32[2,1536,128]{2,1,0:T(8,128)} %get-tuple-element.433, f32[2,1536]{1,0:T(2,128)S(1)} %get-tuple-element.402, bf16[512,2,128]{2,1,0:T(2,128)(2,1)S(1)} %bitcast.113), kind=kOutput, calls=%fused_computation.13.clone.1 | convolution fusion | flops 409731072 | bytes 9724416 | tf_op jit(solution)/shard_map/while/body/gqk,kgd->gqd/dot_general | solution.py:39
  103.5 6.3 %fusion.57 = f32[2,1536,128]{2,1,0:T(8,128)} fusion(f32[2,512,1536]{2,1,0:T(8,128)} %copy-done.1, f32[2,1536]{1,0:T(2,128)S(1)} %max.14, pred[512]{0:T(512)(128)(4,1)S(1)} %broadcast_bitcast_fusion.2, f32[2,1536,128]{2,1,0:T(8,128)} %get-tuple-element.433, f32[2,1536]{1,0:T(2,128)S(1)} %get-tuple-element.402, bf16[512,2,128]{2,1,0:T(2,128)(2,1)S(1)} %bitcast.113), kind=kOutput, calls=%fused_computation.13.clone.1 | convolution fusion | flops 409731072 | bytes 9724416 | tf_op jit(solution)/shard_map/while/body/gqk,kgd->gqd/dot_general | solution.py:39
  119.7 6.3 %fusion.57 = f32[2,1536,128]{2,1,0:T(8,128)} fusion(f32[2,512,1536]{2,1,0:T(8,128)} %copy-done.1, f32[2,1536]{1,0:T(2,128)S(1)} %max.14, pred[512]{0:T(512)(128)(4,1)S(1)} %broadcast_bitcast_fusion.2, f32[2,1536,128]{2,1,0:T(8,128)} %get-tuple-element.433, f32[2,1536]{1,0:T(2,128)S(1)} %get-tuple-element.402, bf16[512,2,128]{2,1,0:T(2,128)(2,1)S(1)} %bitcast.113), kind=kOutput, calls=%fused_computation.13.clone.1 | convolution fusion | flops 409731072 | bytes 9724416 | tf_op jit(solution)/shard_map/while/body/gqk,kgd->gqd/dot_general | solution.py:39
  135.9 6.3 %fusion.57 = f32[2,1536,128]{2,1,0:T(8,128)} fusion(f32[2,512,1536]{2,1,0:T(8,128)} %copy-done.1, f32[2,1536]{1,0:T(2,128)S(1)} %max.14, pred[512]{0:T(512)(128)(4,1)S(1)} %broadcast_bitcast_fusion.2, f32[2,1536,128]{2,1,0:T(8,128)} %get-tuple-element.433, f32[2,1536]{1,0:T(2,128)S(1)} %get-tuple-element.402, bf16[512,2,128]{2,1,0:T(2,128)(2,1)S(1)} %bitcast.113), kind=kOutput, calls=%fused_computation.13.clone.1 | convolution fusion | flops 409731072 | bytes 9724416 | tf_op jit(solution)/shard_map/while/body/gqk,kgd->gqd/dot_general | solution.py:39
  152.1 6.3 %fusion.57 = f32[2,1536,128]{2,1,0:T(8,128)} fusion(f32[2,512,1536]{2,1,0:T(8,128)} %copy-done.1, f32[2,1536]{1,0:T(2,128)S(1)} %max.14, pred[512]{0:T(512)(128)(4,1)S(1)} %broadcast_bitcast_fusion.2, f32[2,1536,128]{2,1,0:T(8,128)} %get-tuple-element.433, f32[2,1536]{1,0:T(2,128)S(1)} %get-tuple-element.402, bf16[512,2,128]{2,1,0:T(2,128)(2,1)S(1)} %bitcast.113), kind=kOutput, calls=%fused_computation.13.clone.1 | convolution fusion | flops 409731072 | bytes 9724416 | tf_op jit(solution)/shard_map/while/body/gqk,kgd->gqd/dot_general | solution.py:39
  168.7 4.9 %all-to-all-start.3 = ((f32[1,768,520]{2,0,1:T(1,128)}), f32[1,768,520]{2,0,1:T(1,128)}, u32[]{:S(2)}, u32[]{:S(2)}) async-start(f32[1,768,520]{2,0,1:T(1,128)} %copy.61), calls=%async_computation.3 | async-start | bytes 3932160 | tf_op jit(solution)/shard_map/all_to_all | solution.py:21
  176.5 94.4 %while.33 = (s32[]{:T(128)}, f32[2,1536]{1,0:T(2,128)S(1)}, f32[2,1536]{1,0:T(2,128)S(1)}, f32[2,1536,128]{2,1,0:T(8,128)S(1)}, bf16[4096,2,128]{2,1,0:T(2,128)(...) while((s32[]{:T(128)}, f32[2,1536]{1,0:T(2,128)S(1)}, ...), condition=%wide.region_3.0_spmd.clone, body=%wide.region_0.0_spmd.clone.sunk | while | flops 819084288 | bytes 49742020 | solution.py:63
  181.6 4.0 %fusion.62 = f32[2,1536]{1,0:T(2,128)S(1)} fusion(f32[2,512,1536]{2,1,0:T(8,128)} %get-tuple-element.412, f32[2,1536]{1,0:T(2,128)S(1)} %fusion.61), kind=kLoop, calls=%fused_computation.29.clone.1 | loop fusion | flops 4715520 | bytes 6316032 | tf_op jit(solution)/shard_map/while/body/eval_jaxpr/reduce_sum | solution.py:38
  193.4 4.0 %fusion.62 = f32[2,1536]{1,0:T(2,128)S(1)} fusion(f32[2,512,1536]{2,1,0:T(8,128)} %get-tuple-element.412, f32[2,1536]{1,0:T(2,128)S(1)} %fusion.61), kind=kLoop, calls=%fused_computation.29.clone.1 | loop fusion | flops 4715520 | bytes 6316032 | tf_op jit(solution)/shard_map/while/body/eval_jaxpr/reduce_sum | solution.py:38
  205.2 4.0 %fusion.62 = f32[2,1536]{1,0:T(2,128)S(1)} fusion(f32[2,512,1536]{2,1,0:T(8,128)} %get-tuple-element.412, f32[2,1536]{1,0:T(2,128)S(1)} %fusion.61), kind=kLoop, calls=%fused_computation.29.clone.1 | loop fusion | flops 4715520 | bytes 6316032 | tf_op jit(solution)/shard_map/while/body/eval_jaxpr/reduce_sum | solution.py:38
  217.0 4.0 %fusion.62 = f32[2,1536]{1,0:T(2,128)S(1)} fusion(f32[2,512,1536]{2,1,0:T(8,128)} %get-tuple-element.412, f32[2,1536]{1,0:T(2,128)S(1)} %fusion.61), kind=kLoop, calls=%fused_computation.29.clone.1 | loop fusion | flops 4715520 | bytes 6316032 | tf_op jit(solution)/shard_map/while/body/eval_jaxpr/reduce_sum | solution.py:38
  228.8 4.0 %fusion.62 = f32[2,1536]{1,0:T(2,128)S(1)} fusion(f32[2,512,1536]{2,1,0:T(8,128)} %get-tuple-element.412, f32[2,1536]{1,0:T(2,128)S(1)} %fusion.61), kind=kLoop, calls=%fused_computation.29.clone.1 | loop fusion | flops 4715520 | bytes 6316032 | tf_op jit(solution)/shard_map/while/body/eval_jaxpr/reduce_sum | solution.py:38
  240.6 4.0 %fusion.62 = f32[2,1536]{1,0:T(2,128)S(1)} fusion(f32[2,512,1536]{2,1,0:T(8,128)} %get-tuple-element.412, f32[2,1536]{1,0:T(2,128)S(1)} %fusion.61), kind=kLoop, calls=%fused_computation.29.clone.1 | loop fusion | flops 4715520 | bytes 6316032 | tf_op jit(solution)/shard_map/while/body/eval_jaxpr/reduce_sum | solution.py:38
  252.4 4.0 %fusion.62 = f32[2,1536]{1,0:T(2,128)S(1)} fusion(f32[2,512,1536]{2,1,0:T(8,128)} %get-tuple-element.412, f32[2,1536]{1,0:T(2,128)S(1)} %fusion.61), kind=kLoop, calls=%fused_computation.29.clone.1 | loop fusion | flops 4715520 | bytes 6316032 | tf_op jit(solution)/shard_map/while/body/eval_jaxpr/reduce_sum | solution.py:38
  264.2 4.0 %fusion.62 = f32[2,1536]{1,0:T(2,128)S(1)} fusion(f32[2,512,1536]{2,1,0:T(8,128)} %get-tuple-element.412, f32[2,1536]{1,0:T(2,128)S(1)} %fusion.61), kind=kLoop, calls=%fused_computation.29.clone.1 | loop fusion | flops 4715520 | bytes 6316032 | tf_op jit(solution)/shard_map/while/body/eval_jaxpr/reduce_sum | solution.py:38
  276.9 9.1 %all-to-all-start.1 = ((f32[1,768,520]{2,0,1:T(1,128)}), f32[1,768,520]{2,0,1:T(1,128)}, u32[]{:S(2)}, u32[]{:S(2)}) async-start(f32[1,768,520]{2,0,1:T(1,128)} %copy.55), calls=%async_computation.1 | async-start | bytes 3932160 | tf_op jit(solution)/shard_map/all_to_all | solution.py:21
  292.7 39.2 %all-to-all-done.1 = f32[1,768,520]{2,0,1:T(1,128)} async-done(((f32[1,768,520]{2,0,1:T(1,128)}), f32[1,768,520]{2,0,1:T(1,128)}, u32[]{:S(2)}, u32[]{:S(2)}) %all-to-all-start.1) | async-done | bytes 1597472 | tf_op jit(solution)/shard_map/all_to_all | solution.py:21
  (223 shorter events, 179.1 us)
Async XLA Ops:
  0.6 9.5 %copy-start.2 = (bf16[96,4096]{1,0:T(8,128)(2,1)S(1)}, bf16[96,4096]{1,0:T(8,128)(2,1)}, u32[]{:S(2)}) copy-start(bf16[96,4096]{1,0:T(8,128)(2,1)} %param.10) | copy-start | bytes 2359300
  2.8 18.8 %all-to-all-start.2 = ((bf16[96,8,512]{2,0,1:T(8,128)(2,1)}), bf16[96,8,512]{2,0,1:T(8,128)(2,1)S(1)}, u32[]{:S(2)}, u32[]{:S(2)}) async-start(bf16[96,8,512]{2,0,1:T(8,128)(2,1)} %bitcast.78), calls=%async_computation.2 | async-start | bytes 1572864 | tf_op jit(solution)/shard_map/all_to_all | solution.py:108
  21.6 147.1 %all-to-all-start = ((bf16[96,8,512]{2,0,1:T(8,128)(2,1)}), bf16[96,8,512]{2,0,1:T(8,128)(2,1)}, u32[]{:S(2)}, u32[]{:S(2)}) async-start(bf16[96,8,512]{2,0,1:T(8,128)(2,1)} %bitcast.79), calls=%async_computation | async-start | bytes 1572864 | tf_op jit(solution)/shard_map/all_to_all | solution.py:107
  26.9 1.8 copy-start.5
  33.2 2.7 copy-start.1
  49.5 2.7 copy-start.1
  65.7 2.7 copy-start.1
  81.9 2.7 copy-start.1
  98.1 2.7 copy-start.1
  114.3 2.7 copy-start.1
  130.5 2.7 copy-start.1
  146.7 2.7 copy-start.1
  168.7 108.1 %all-to-all-start.3 = ((f32[1,768,520]{2,0,1:T(1,128)}), f32[1,768,520]{2,0,1:T(1,128)}, u32[]{:S(2)}, u32[]{:S(2)}) async-start(f32[1,768,520]{2,0,1:T(1,128)} %copy.61), calls=%async_computation.3 | async-start | bytes 3932160 | tf_op jit(solution)/shard_map/all_to_all | solution.py:21
  181.6 4.6 %copy-start = (f32[2,512,1536]{2,1,0:T(8,128)S(1)}, f32[2,512,1536]{2,1,0:T(8,128)}, u32[]{:S(2)}) copy-start(f32[2,512,1536]{2,1,0:T(8,128)} %get-tuple-element.412) | copy-start | bytes 18874372 | tf_op jit(solution)/shard_map/while
  193.4 4.6 %copy-start = (f32[2,512,1536]{2,1,0:T(8,128)S(1)}, f32[2,512,1536]{2,1,0:T(8,128)}, u32[]{:S(2)}) copy-start(f32[2,512,1536]{2,1,0:T(8,128)} %get-tuple-element.412) | copy-start | bytes 18874372 | tf_op jit(solution)/shard_map/while
  205.2 4.6 %copy-start = (f32[2,512,1536]{2,1,0:T(8,128)S(1)}, f32[2,512,1536]{2,1,0:T(8,128)}, u32[]{:S(2)}) copy-start(f32[2,512,1536]{2,1,0:T(8,128)} %get-tuple-element.412) | copy-start | bytes 18874372 | tf_op jit(solution)/shard_map/while
  217.0 4.6 %copy-start = (f32[2,512,1536]{2,1,0:T(8,128)S(1)}, f32[2,512,1536]{2,1,0:T(8,128)}, u32[]{:S(2)}) copy-start(f32[2,512,1536]{2,1,0:T(8,128)} %get-tuple-element.412) | copy-start | bytes 18874372 | tf_op jit(solution)/shard_map/while
  228.8 4.6 %copy-start = (f32[2,512,1536]{2,1,0:T(8,128)S(1)}, f32[2,512,1536]{2,1,0:T(8,128)}, u32[]{:S(2)}) copy-start(f32[2,512,1536]{2,1,0:T(8,128)} %get-tuple-element.412) | copy-start | bytes 18874372 | tf_op jit(solution)/shard_map/while
  240.6 4.6 %copy-start = (f32[2,512,1536]{2,1,0:T(8,128)S(1)}, f32[2,512,1536]{2,1,0:T(8,128)}, u32[]{:S(2)}) copy-start(f32[2,512,1536]{2,1,0:T(8,128)} %get-tuple-element.412) | copy-start | bytes 18874372 | tf_op jit(solution)/shard_map/while
  252.4 4.6 %copy-start = (f32[2,512,1536]{2,1,0:T(8,128)S(1)}, f32[2,512,1536]{2,1,0:T(8,128)}, u32[]{:S(2)}) copy-start(f32[2,512,1536]{2,1,0:T(8,128)} %get-tuple-element.412) | copy-start | bytes 18874372 | tf_op jit(solution)/shard_map/while
  264.2 4.6 %copy-start = (f32[2,512,1536]{2,1,0:T(8,128)S(1)}, f32[2,512,1536]{2,1,0:T(8,128)}, u32[]{:S(2)}) copy-start(f32[2,512,1536]{2,1,0:T(8,128)} %get-tuple-element.412) | copy-start | bytes 18874372 | tf_op jit(solution)/shard_map/while
  276.9 55.1 %all-to-all-start.1 = ((f32[1,768,520]{2,0,1:T(1,128)}), f32[1,768,520]{2,0,1:T(1,128)}, u32[]{:S(2)}, u32[]{:S(2)}) async-start(f32[1,768,520]{2,0,1:T(1,128)} %copy.55), calls=%async_computation.1 | async-start | bytes 3932160 | tf_op jit(solution)/shard_map/all_to_all | solution.py:21
  338.2 0.7 copy-start.4
  338.2 0.8 copy-start.3
where the time goes:
time: 342 us; the launch traced here: 340 us
  matrix products  105 us (31%)
  local copies, waits for them, and re-layouts  102 us (30%)
  other arithmetic  55.1 us (16%)
  waiting for transfers between devices  49.7 us (15%)
  starting transfers between devices  25.7 us (8%)
    dot_general x16, matrix products, absorb(): jnp.einsum('gqk,kgd->gqd', weights.astype(jnp.bfloat16), value_part, pref...  67.3 us
    reduce_sum x16, other arithmetic, absorb(): row_total = row_total * factor + jnp.sum(weights, axis=2)  43.7 us
    all_to_all x2, waiting for transfers between devices, in_one_piece(): lax.all_to_all(both, axis, split_axis=split_dim, concat_axis=concat_dim,...  39.2 us
    dot_general x16, matrix products, absorb(): jnp.einsum('gqd,kgd->gqk', head_queries, key_part, preferred_element_type...  37.4 us
    gather x8, local copies, waits for them, and re-layouts, absorb_group(): value_part = value_blocks[block_ids].reshape(per_turn * BLK, kv_local, HD)  21.3 us
    gather x8, local copies, waits for them, and re-layouts, absorb_group(): key_part = key_blocks[block_ids].reshape(per_turn * BLK, kv_local, HD)  21.3 us
    all_to_all x2, starting transfers between devices, in_one_piece(): lax.all_to_all(both, axis, split_axis=split_dim, concat_axis=concat_dim,...  14 us
    while x48, local copies, waits for them, and re-layouts  13.9 us
  transfers between devices with their start and end apart: 4, of which 2 were waited for; matrix products, arithmetic and copies ran while one was open for 70% of the time, Pallas kernels for 0%

commit v1 on v0

v1 whole, which is shorter than its diff:
```python
import functools

import jax
import jax.numpy as jnp
from jax import lax
from jax.experimental import pallas as pl
from jax.experimental.pallas import tpu as pltpu
from jax.sharding import PartitionSpec as P

HD = 128
BLK = 128
F32 = jnp.float32
BF16 = jnp.bfloat16
SCALE = 168 ** -0.5 * 1.4426950408889634
NEG = -1e30
MESH = pl.DeviceIdType.MESH

KV = 2
KEYS = 4096
ROWS = 1536
QT = 256
TILES = ROWS // QT
CK = 1024
NB = KEYS // CK
NX, NY, NZ = 4, 4, 8
GRP = ROWS // NY
OWN = GRP // NZ
VROWS = HD + 16

Q_HOPS = ((0, 1), (1, 0), (1, 1), (3, 0), (3, 1), (2, 0), (2, 1))


def head_at(me, dx, dc):
    x, c = me // 2, me % 2
    return ((x + dx) % NX) * 2 + (c + dc) % 2


def ctx_at(y, z):
    return (y % NY) * NZ + z % NZ


def remote(src, dst, send_sem, recv_sem, **where):
    return pltpu.make_async_remote_copy(
        src_ref=src, dst_ref=dst, send_sem=send_sem, recv_sem=recv_sem, device_id=where, device_id_type=MESH
    )


def prep_keys(kraw, kx, stage):
    n = stage.shape[0]

    def step(i, c):
        stage[...] = kraw[pl.ds(i * n, n), :].astype(F32)
        for h in range(KV):
            k = stage[pl.ds(h, n // 2, stride=2), :].astype(BF16)
            rows = pl.ds(i * (n // 2), n // 2)
            kx[h, rows, 0:HD] = k
            kx[h, rows, HD : 2 * HD] = k
        return c

    lax.fori_loop(0, KEYS * KV // n, step, 0)


def prep_values(vraw, vt, stage):
    n = stage.shape[0]

    def step(i, c):
        stage[...] = vraw[pl.ds(i * n, n), :].astype(F32)
        for h in range(KV):
            v = stage[pl.ds(h, n // 2, stride=2), :].astype(BF16)
            vt[h, 0:HD, pl.ds(pl.multiple_of(i * (n // 2), n // 2), n // 2)] = v.T
        return c

    lax.fori_loop(0, KEYS * KV // n, step, 0)
    for h in range(KV):
        vt[h, HD:VROWS, :] = jnp.ones((VROWS - HD, KEYS), BF16)


def prep_queries(qraw, qx, blk, place):
    def step(hs, c):
        x = qraw[blk, hs].astype(F32) * SCALE
        rows = pl.ds(pl.multiple_of(place(hs) * (4 * OWN), 64), 4 * OWN)
        for h in range(KV):
            a = x[:, h * 256 : h * 256 + 128]
            b = x[:, h * 256 + 128 : h * 256 + 256]
            pieces = []
            for j in range(4):
                pieces += [a[j * 24 : j * 24 + 24], b[j * 24 : j * 24 + 24]]
            full = jnp.concatenate(pieces, axis=0)
            hi = full.astype(BF16)
            qx[blk, h, rows, 0:HD] = hi
            qx[blk, h, rows, HD : 2 * HD] = (full - hi.astype(F32)).astype(BF16)
        return c

    lax.fori_loop(0, 8, step, 0)


def scores_step(i, q, kx, h, s_ref, bias, blk, top):
    s = lax.dot_general(
        kx[h, pl.ds(i * CK, CK), :], q, (((1,), (1,)), ((), ())), preferred_element_type=F32
    )
    s_ref[pl.ds(i * CK, CK), :] = s
    for b in range(CK // BLK):
        part = s[b * BLK : (b + 1) * BLK].reshape(BLK // 8, 8, QT)
        top = jnp.maximum(top, jnp.max(part, axis=0) + bias[blk, pl.ds(i * (CK // BLK) + b, 1), :])
    return top


def values_step(i, vt, h, s_ref, bias, blk, top, total):
    pieces = []
    for b in range(CK // BLK):
        shift = top - bias[blk, pl.ds(i * (CK // BLK) + b, 1), :]
        pieces.append(jnp.exp2(s_ref[pl.ds(i * CK + b * BLK, BLK), :] - shift).astype(BF16))
    p = jnp.concatenate(pieces, axis=0)
    d = lax.dot_general(
        vt[h, :, pl.ds(i * CK, CK)], p, (((1,), (0,)), ((), ())), preferred_element_type=F32
    )
    return d if total is None else total + d


def sweep(blk, kx, vt, qx, bias, obuf, lse, s0, s1):
    n = KV * TILES

    def q_tile(t):
        return qx[blk, t // TILES, pl.ds(pl.multiple_of((t % TILES) * QT, QT), QT), :]

    def first(t, s):
        q = q_tile(t)
        top = jnp.full((8, QT), NEG, F32)
        for i in range(NB):
            top = scores_step(i, q, kx, t // TILES, s, bias, blk, top)
        return jnp.max(top, axis=0, keepdims=True)

    def both(ta, sa, tb, sb, m):
        q = q_tile(ta)
        top = jnp.full((8, QT), NEG, F32)
        total = None
        for i in range(NB):
            top = scores_step(i, q, kx, ta // TILES, sa, bias, blk, top)
            total = values_step(i, vt, tb // TILES, sb, bias, blk, m, total)
        norm = total[HD : HD + 1, :]
        h, cols = tb // TILES, pl.ds(pl.multiple_of((tb % TILES) * QT, QT), QT)
        obuf[blk, h, cols, :] = (total[0:HD, :] * (1.0 / norm)).T.astype(BF16)
        lse[blk, h, :, cols] = m + jnp.log2(norm)
        return jnp.max(top, axis=0, keepdims=True)

    def step(i, m):
        m = both(2 * i + 1, s1, 2 * i, s0, m)
        return both(jnp.minimum(2 * i + 2, n - 1), s0, 2 * i + 1, s1, m)

    lax.fori_loop(0, n // 2, step, first(0, s0))


def combine_y(blk, obuf, lse, r1, l1, c1, lz):
    rows = []
    for h in range(KV):
        ls = [lse[blk, h, :, 0:GRP]] + [l1[blk, k, h] for k in range(NY - 1)]
        m = functools.reduce(jnp.maximum, ls)
        ws = [jnp.exp2(l - m) for l in ls]
        total = functools.reduce(jnp.add, ws)
        rows += [w / total for w in ws]
        both = m + jnp.log2(total)
        for z in range(NZ):
            lz[blk, z, h : h + 1, 0:OWN] = both[:, z * OWN : (z + 1) * OWN]
    w = jnp.concatenate(rows, axis=0).T
    for h in range(KV):
        acc = obuf[blk, h, 0:GRP, :].astype(F32) * w[:, h * NY : h * NY + 1]
        for k in range(NY - 1):
            acc += r1[blk, k, h].astype(F32) * w[:, h * NY + k + 1 : h * NY + k + 2]
        c1[blk, h] = acc.astype(BF16)


def combine_z(blk, z, c1, lz, r2, l2, out_ref):
    mine = pl.ds(pl.multiple_of(z * OWN, 16), OWN)
    ls = [lz[blk, z]] + [l2[blk, j] for j in range(NZ - 1)]
    m = functools.reduce(jnp.maximum, ls)
    ws = [jnp.exp2(l - m) for l in ls]
    total = functools.reduce(jnp.add, ws)
    w = jnp.concatenate([x / total for x in ws], axis=0).T
    for h in range(KV):
        acc = c1[blk, h, mine, :].astype(F32) * w[0:OWN, h : h + 1]
        for j in range(NZ - 1):
            col = (j + 1) * KV + h
            acc += r2[blk, j, h].astype(F32) * w[0:OWN, col : col + 1]
        for g in range(2):
            at = (h * 2 + g) * HD
            out_ref[:, at : at + HD] = acc[g * 24 : (g + 1) * 24].astype(BF16)


def kernel(
    q0, q1, k_hbm, v_hbm, kept_ref, count_ref, out0, out1,
    kraw, vraw, qraw, kx, vt, stage, qx, bias, s0, s1, obuf, lse, r1, l1, c1, lz, r2, l2,
    local, qs_sem, qr_sem, ys_sem, yr_sem, yls_sem, ylr_sem, zs_sem, zr_sem, zls_sem, zlr_sem,
):
    me, ctx = lax.axis_index("head"), lax.axis_index("ctx")
    y, z = ctx // NZ, ctx % NZ
    outs = (out0, out1)
    kcopy = pltpu.make_async_copy(k_hbm, kraw, local.at[0])
    vcopy = pltpu.make_async_copy(v_hbm, vraw, local.at[1])
    kcopy.start()
    vcopy.start()
    own = []
    cols = pl.ds(pl.multiple_of(me * 512, 512), 512)
    for blk, q in enumerate((q0, q1)):
        own.append(pltpu.make_async_copy(q.at[:, cols], qraw.at[blk, me], local.at[2 + blk]))
        own[-1].start()

    barrier = pltpu.get_barrier_semaphore()
    for dx, dc in Q_HOPS:
        pl.semaphore_signal(barrier, inc=1, device_id={"head": head_at(me, dx, dc)}, device_id_type=MESH)
    for k in range(1, NY):
        pl.semaphore_signal(barrier, inc=1, device_id={"ctx": ctx_at(y + k, z)}, device_id_type=MESH)
    for j in range(1, NZ):
        pl.semaphore_signal(barrier, inc=1, device_id={"ctx": ctx_at(y, z + j)}, device_id_type=MESH)
    pl.semaphore_wait(barrier, len(Q_HOPS) + NY - 1 + NZ - 1)

    sends = []

    def q_copy(blk, n, dest, source):
        to = pl.ds(pl.multiple_of(dest * 512, 512), 512)
        return remote(
            (q0, q1)[blk].at[:, to], qraw.at[blk, source], qs_sem.at[blk, n], qr_sem.at[blk, n], head=dest
        )

    for blk in range(2):
        for n, (dx, dc) in enumerate(Q_HOPS):
            copy = q_copy(blk, n, head_at(me, dx, dc), me)
            copy.start()
            sends.append(copy)

    def wait_queries(blk):
        own[blk].wait()
        for n, (dx, dc) in enumerate(Q_HOPS):
            q_copy(blk, n, me, head_at(me, NX - dx, dc)).wait_recv()

    flags = jnp.where(
        (kept_ref[...] == lax.broadcasted_iota(jnp.int32, (32, 32), 0))
        & (lax.broadcasted_iota(jnp.int32, (32, 32), 1) < count_ref[0]),
        1.0, 0.0,
    )
    kept = jnp.max(flags, axis=1, keepdims=True)
    bias[0] = jnp.zeros((32, QT), F32)
    bias[1] = jnp.broadcast_to((1.0 - kept) * NEG, (32, QT))
    lz[...] = jnp.zeros(lz.shape, F32)

    kcopy.wait()
    prep_keys(kraw, kx, stage)
    vcopy.wait()
    prep_values(vraw, vt, stage)

    def place(hs):
        return ((hs // 2 + NY - y) % NY) * 2 + hs % 2

    def y_copies(blk):
        made = []
        for k in range(1, NY):
            at = pl.ds(k * GRP, GRP)
            dest = ctx_at(y + k, z)
            made.append(remote(
                obuf.at[blk, :, at, :], r1.at[blk, k - 1], ys_sem.at[blk, k - 1], yr_sem.at[blk, k - 1], ctx=dest
            ))
            made.append(remote(
                lse.at[blk, :, :, at], l1.at[blk, k - 1], yls_sem.at[blk, k - 1], ylr_sem.at[blk, k - 1], ctx=dest
            ))
        return made

    def z_copies(blk):
        made = []
        for j in range(1, NZ):
            to = (z + j) % NZ
            at = pl.ds(pl.multiple_of(to * OWN, 16), OWN)
            dest = ctx_at(y, to)
            made.append(remote(
                c1.at[blk, :, at, :], r2.at[blk, j - 1], zs_sem.at[blk, j - 1], zr_sem.at[blk, j - 1], ctx=dest
            ))
            made.append(remote(
                lz.at[blk, to], l2.at[blk, j - 1], zls_sem.at[blk, j - 1], zlr_sem.at[blk, j - 1], ctx=dest
            ))
        return made

    def begin(copies):
        for copy in copies:
            copy.start()
        sends.extend(copies)
        return copies

    def arrive(copies):
        for copy in copies:
            copy.wait_recv()

    wait_queries(0)
    prep_queries(qraw, qx, 0, place)
    sweep(0, kx, vt, qx, bias, obuf, lse, s0, s1)
    ya = begin(y_copies(0))
    wait_queries(1)
    prep_queries(qraw, qx, 1, place)
    sweep(1, kx, vt, qx, bias, obuf, lse, s0, s1)
    yb = begin(y_copies(1))
    arrive(ya)
    combine_y(0, obuf, lse, r1, l1, c1, lz)
    za = begin(z_copies(0))
    arrive(yb)
    combine_y(1, obuf, lse, r1, l1, c1, lz)
    zb = begin(z_copies(1))
    arrive(za)
    combine_z(0, z, c1, lz, r2, l2, outs[0])
    arrive(zb)
    combine_z(1, z, c1, lz, r2, l2, outs[1])
    for copy in sends:
        copy.wait_send()


def shards(q_first, q_second, k_cache, v_cache, kept_blocks, kept_count):
    anyspace = pl.BlockSpec(memory_space=pl.ANY)
    vmem = pl.BlockSpec(memory_space=pltpu.VMEM)
    dma = pltpu.SemaphoreType.DMA
    out = jax.ShapeDtypeStruct((24, 512), BF16)
    return pl.pallas_call(
        kernel,
        out_shape=(out, out),
        in_specs=[anyspace] * 4 + [vmem, pl.BlockSpec(memory_space=pltpu.SMEM)],
        out_specs=(vmem, vmem),
        scratch_shapes=[
            pltpu.VMEM((KEYS * KV, HD), BF16),
            pltpu.VMEM((KEYS * KV, HD), BF16),
            pltpu.VMEM((2, 8, 96, 512), BF16),
            pltpu.VMEM((KV, KEYS, 2 * HD), BF16),
            pltpu.VMEM((KV, VROWS, KEYS), BF16),
            pltpu.VMEM((1024, HD), F32),
            pltpu.VMEM((2, KV, ROWS, 2 * HD), BF16),
            pltpu.VMEM((2, 32, QT), F32),
            pltpu.VMEM((KEYS, QT), F32),
            pltpu.VMEM((KEYS, QT), F32),
            pltpu.VMEM((2, KV, ROWS, HD), BF16),
            pltpu.VMEM((2, KV, 1, ROWS), F32),
            pltpu.VMEM((2, NY - 1, KV, GRP, HD), BF16),
            pltpu.VMEM((2, NY - 1, KV, 1, GRP), F32),
            pltpu.VMEM((2, KV, GRP, HD), BF16),
            pltpu.VMEM((2, NZ, KV, 128), F32),
            pltpu.VMEM((2, NZ - 1, KV, OWN, HD), BF16),
            pltpu.VMEM((2, NZ - 1, KV, 128), F32),
            dma((4,)),
            dma((2, 7)), dma((2, 7)),
            dma((2, 3)), dma((2, 3)), dma((2, 3)), dma((2, 3)),
            dma((2, 7)), dma((2, 7)), dma((2, 7)), dma((2, 7)),
        ],
        compiler_params=pltpu.CompilerParams(
            collective_id=0, has_side_effects=True, vmem_limit_bytes=60 * 1024 * 1024
        ),
    )(
        q_first, q_second,
        k_cache.reshape(KEYS * KV, HD), v_cache.reshape(KEYS * KV, HD),
        kept_blocks, kept_count,
    )


def solution(mesh):
    placed = (
        P("head", None),
        P("head", None),
        P("ctx", "head", None),
        P("ctx", "head", None),
        P("ctx", None),
        P("ctx"),
    )
    return jax.shard_map(
        shards,
        mesh=mesh,
        in_specs=placed,
        out_specs=(P("ctx", "head"), P("ctx", "head")),
        check_vma=False,
    )
```

time: 342 us -> 72.6 us (0.21)
  matrix products: 105 us -> 0 us
  local copies, waits for them, and re-layouts: 102 us -> 2.69 us
  Pallas kernels: 0 us -> 68.4 us
  other arithmetic: 55.1 us -> 0 us
  waiting for transfers between devices: 49.7 us -> 0 us
  starting transfers between devices: 25.7 us -> 0 us
    dot_general x32 -> x0, matrix products: 105 us -> none  [the longest x16 67.3 us: absorb(): jnp.einsum('gqk,kgd->gqd', weights.astype(jnp.bfloat16), value_part, pref...]
    pallas_call x0 -> x1, Pallas kernels: none -> 68.4 us  [shards(): pl.pallas_call(kernel, out_shape=(out, out), in_specs=[anyspace] * 4 + [v...]
    all_to_all x4 -> x0, waiting for transfers between devices: 49.7 us -> none  [the longest x2 39.2 us: in_one_piece(): lax.all_to_all(both, axis, split_axis=split_dim, concat_axis=concat_dim,...]
    reduce_sum x20 -> x0, other arithmetic: 46.2 us -> none  [the longest x16 43.7 us: absorb(): row_total = row_total * factor + jnp.sum(weights, axis=2)]
    gather x16 -> x0, local copies, waits for them, and re-layouts: 42.6 us -> none  [the longest x8 21.3 us: absorb_group(): value_part = value_blocks[block_ids].reshape(per_turn * BLK, kv_local, HD)]
    all_to_all x4 -> x0, starting transfers between devices: 25.7 us -> none  [the longest x2 14 us: in_one_piece(): lax.all_to_all(both, axis, split_axis=split_dim, concat_axis=concat_dim,...]
    while x48 -> x0, local copies, waits for them, and re-layouts: 13.9 us -> none
    dynamic_slice x8 -> x0, local copies, waits for them, and re-layouts: 11.2 us -> none  [absorb_block(): lax.dynamic_slice_in_dim(values, step_index * block_keys, block_keys, 0)]
  transfers between devices with their start and end apart: 4 -> 0, of which waited for: 2 -> 0; matrix products, arithmetic and copies ran while one was open for 70% -> 0% of each run, Pallas kernels for 0% -> 0%
where the time goes in v1:
time: 72.6 us; the launch traced here: 72.4 us
  Pallas kernels  68.4 us (94%)
  local copies, waits for them, and re-layouts  2.69 us (4%)
  between operations  1.29 us (2%)
    pallas_call x1, Pallas kernels, shards(): pl.pallas_call(kernel, out_shape=(out, out), in_specs=[anyspace] * 4 + [v...  68.4 us
    unnamed x2, local copies, waits for them, and re-layouts  2.69 us

profile of v1, /device:TPU:1, one launch (start us, length us, event | category | flops | bytes accessed | tf_op | source)
XLA Modules:
  0.0 72.4 jit_solution(5510670861538186458)
XLA Ops:
  1.3 68.4 %shard_map.77 = (bf16[24,512]{1,0:T(8,128)(2,1)}, bf16[24,512]{1,0:T(8,128)(2,1)}) custom-call(bf16[96,4096]{1,0:T(8,128)(2,1)} %q0.1, bf16[96,4096]{1,0:T(8,128)(2,1)} %q1.1, bf16[8192,128]{1,0:T(8,128)(2,1)} %bitcast.2, bf16[8192,128]{1,0:T(8,128)(2,1)} %bitcast.3, s32[1,32]{1,0:T(1,128)} %kept_ref.1, s32[1]{0:T(128)S(6)} %copy.10.count_ref), custom_call_target="tpu_custom_call" | custom-call | tf_op jit(solution)/shard_map/pallas_call | solution.py:317
  69.7 1.3 %copy.11 = bf16[24,512]{1,0:T(8,128)(2,1)} copy(bf16[24,512]{1,0:T(8,128)(2,1)} %get-tuple-element.4) | data formatting | bytes 49152
  71.0 1.3 %copy.12 = bf16[24,512]{1,0:T(8,128)(2,1)} copy(bf16[24,512]{1,0:T(8,128)(2,1)} %get-tuple-element.5) | data formatting | bytes 49152

commit v2 on v1

v2 whole, which is shorter than its diff:
```python
import functools

import jax
import jax.numpy as jnp
from jax import lax
from jax.experimental import pallas as pl
from jax.experimental.pallas import tpu as pltpu
from jax.sharding import PartitionSpec as P

HD = 128
BLK = 128
F32 = jnp.float32
BF16 = jnp.bfloat16
SCALE = 168 ** -0.5 * 1.4426950408889634
NEG = -1e30
MESH = pl.DeviceIdType.MESH

KV = 2
KEYS = 4096
ROWS = 1536
QT = 256
TILES = ROWS // QT
CK = 1024
NB = KEYS // CK
NX, NY, NZ = 4, 4, 8
GRP = ROWS // NY
OWN = GRP // NZ
VROWS = HD + 16

Q_HOPS = ((0, 1), (1, 0), (1, 1), (3, 0), (3, 1), (2, 0), (2, 1))


def head_at(me, dx, dc):
    x, c = me // 2, me % 2
    return ((x + dx) % NX) * 2 + (c + dc) % 2


def ctx_at(y, z):
    return (y % NY) * NZ + z % NZ


def remote(src, dst, send_sem, recv_sem, **where):
    return pltpu.make_async_remote_copy(
        src_ref=src, dst_ref=dst, send_sem=send_sem, recv_sem=recv_sem, device_id=where, device_id_type=MESH
    )


def prep_keys(kraw, kx, stage):
    n = stage.shape[0]

    def step(i, c):
        stage[...] = kraw[pl.ds(i * n, n), :].astype(F32)
        for h in range(KV):
            k = stage[pl.ds(h, n // 2, stride=2), :].astype(BF16)
            rows = pl.ds(i * (n // 2), n // 2)
            kx[h, rows, 0:HD] = k
            kx[h, rows, HD : 2 * HD] = k
        return c

    lax.fori_loop(0, KEYS * KV // n, step, 0)


def prep_values(vraw, vt, stage):
    n = stage.shape[0]

    def step(i, c):
        stage[...] = vraw[pl.ds(i * n, n), :].astype(F32)
        for h in range(KV):
            v = stage[pl.ds(h, n // 2, stride=2), :].astype(BF16)
            vt[h, 0:HD, pl.ds(pl.multiple_of(i * (n // 2), n // 2), n // 2)] = v.T
        return c

    lax.fori_loop(0, KEYS * KV // n, step, 0)
    for h in range(KV):
        vt[h, HD:VROWS, :] = jnp.ones((VROWS - HD, KEYS), BF16)


def prep_queries(qraw, qx, blk, hs, pos):
    x = qraw[blk, hs].astype(F32) * SCALE
    rows = pl.ds(pl.multiple_of(pos * (4 * OWN), 64), 4 * OWN)
    for h in range(KV):
        a = x[:, h * 256 : h * 256 + 128]
        b = x[:, h * 256 + 128 : h * 256 + 256]
        pieces = []
        for j in range(4):
            pieces += [a[j * 24 : j * 24 + 24], b[j * 24 : j * 24 + 24]]
        full = jnp.concatenate(pieces, axis=0)
        hi = full.astype(BF16)
        qx[blk, h, rows, 0:HD] = hi
        qx[blk, h, rows, HD : 2 * HD] = (full - hi.astype(F32)).astype(BF16)


def scores_step(i, q, kx, h, s_ref, bias, blk, top):
    s = lax.dot_general(
        kx[h, pl.ds(i * CK, CK), :], q, (((1,), (1,)), ((), ())), preferred_element_type=F32
    )
    s_ref[pl.ds(i * CK, CK), :] = s
    for b in range(CK // BLK):
        part = s[b * BLK : (b + 1) * BLK].reshape(BLK // 8, 8, QT)
        top = jnp.maximum(top, jnp.max(part, axis=0) + bias[blk, pl.ds(i * (CK // BLK) + b, 1), :])
    return top


def values_step(i, vt, h, s_ref, bias, blk, top, total):
    pieces = []
    for b in range(CK // BLK):
        shift = top - bias[blk, pl.ds(i * (CK // BLK) + b, 1), :]
        pieces.append(jnp.exp2(s_ref[pl.ds(i * CK + b * BLK, BLK), :] - shift).astype(BF16))
    p = jnp.concatenate(pieces, axis=0)
    d = lax.dot_general(
        vt[h, :, pl.ds(i * CK, CK)], p, (((1,), (0,)), ((), ())), preferred_element_type=F32
    )
    return d if total is None else total + d


def make_tiles(kx, vt, qx, bias, obuf, lse, s0, s1):
    slots = (s0, s1)

    def cols(i):
        return pl.ds(pl.multiple_of((i % TILES) * QT, QT), QT)

    def finish(i, h, total, m):
        norm = total[HD : HD + 1, :]
        obuf[i // TILES, h, cols(i), :] = (total[0:HD, :] * (1.0 / norm)).T.astype(BF16)
        lse[i // TILES, h, :, cols(i)] = m + jnp.log2(norm)

    def run(score=None, value=None, m=None):
        top = jnp.full((8, QT), NEG, F32)
        total = None
        if score is not None:
            ia, ha = score
            q = qx[ia // TILES, ha, cols(ia), :]
        for n in range(NB):
            if score is not None:
                top = scores_step(n, q, kx, ha, slots[ha], bias, ia // TILES, top)
            if value is not None:
                ib, hb = value
                total = values_step(n, vt, hb, slots[hb], bias, ib // TILES, m, total)
        if value is not None:
            finish(ib, hb, total, m)
        return jnp.max(top, axis=0, keepdims=True)

    return run


def combine_y(blk, h, mine, obuf, lse, r1, l1, c1, lz):
    ls = [lse[blk, h, :, mine]] + [l1[blk, k, h] for k in range(NY - 1)]
    m = functools.reduce(jnp.maximum, ls)
    ws = [jnp.exp2(l - m) for l in ls]
    total = functools.reduce(jnp.add, ws)
    both = m + jnp.log2(total)
    for z in range(NZ):
        lz[blk, z, h, :, 0:OWN] = both[:, z * OWN : (z + 1) * OWN]
    w = jnp.concatenate([w / total for w in ws] * 2, axis=0).T
    acc = obuf[blk, h, mine, :].astype(F32) * w[:, 0:1]
    for k in range(NY - 1):
        acc += r1[blk, k, h].astype(F32) * w[:, k + 1 : k + 2]
    c1[blk, h] = acc.astype(BF16)


def combine_z(blk, h, z, c1, lz, r2, l2, out_ref):
    mine = pl.ds(pl.multiple_of(z * OWN, 16), OWN)
    ls = [lz[blk, z, h]] + [l2[blk, j, h] for j in range(NZ - 1)]
    m = functools.reduce(jnp.maximum, ls)
    ws = [jnp.exp2(l - m) for l in ls]
    total = functools.reduce(jnp.add, ws)
    w = jnp.concatenate([x / total for x in ws], axis=0).T
    acc = c1[blk, h, mine, :].astype(F32) * w[0:OWN, 0:1]
    for j in range(NZ - 1):
        acc += r2[blk, j, h].astype(F32) * w[0:OWN, j + 1 : j + 2]
    for g in range(2):
        at = (h * 2 + g) * HD
        out_ref[blk, :, at : at + HD] = acc[g * 24 : (g + 1) * 24].astype(BF16)


def kernel(
    q0, q1, k_hbm, v_hbm, kept_ref, count_ref, out,
    kraw, vraw, qraw, kx, vt, stage, qx, bias, s0, s1, obuf, lse, r1, l1, c1, lz, r2, l2,
    local, qs_sem, qr_sem, ys_sem, yr_sem, yls_sem, ylr_sem, zs_sem, zr_sem, zls_sem, zlr_sem, near, far,
):
    me, ctx = lax.axis_index("head"), lax.axis_index("ctx")
    x, y, z = me // 2, ctx // NZ, ctx % NZ

    barrier = pltpu.get_barrier_semaphore()
    for dx, dc in Q_HOPS:
        pl.semaphore_signal(barrier, inc=1, device_id={"head": head_at(me, dx, dc)}, device_id_type=MESH)
    for k in range(1, NY):
        pl.semaphore_signal(barrier, inc=1, device_id={"ctx": ctx_at(y + k, z)}, device_id_type=MESH)
    for j in (1, NZ - 1):
        pl.semaphore_signal(barrier, inc=1, device_id={"ctx": ctx_at(y, z + j)}, device_id_type=MESH)

    kcopy = pltpu.make_async_copy(k_hbm, kraw, local.at[0])
    vcopy = pltpu.make_async_copy(v_hbm, vraw, local.at[1])
    own = []
    cols = pl.ds(pl.multiple_of(me * 512, 512), 512)
    for blk, q in enumerate((q0, q1)):
        own.append(pltpu.make_async_copy(q.at[:, cols], qraw.at[blk, me], local.at[2 + blk]))
    own[0].start()
    kcopy.start()
    vcopy.start()
    own[1].start()

    pl.semaphore_wait(barrier, len(Q_HOPS) + NY - 1 + 2)

    sends = []

    def q_copy(blk, n, dest, source):
        to = pl.ds(pl.multiple_of(dest * 512, 512), 512)
        return remote(
            (q0, q1)[blk].at[:, to], qraw.at[blk, source], qs_sem.at[blk, n], qr_sem.at[blk, n], head=dest
        )

    for blk in range(2):
        for n, (dx, dc) in enumerate(Q_HOPS):
            copy = q_copy(blk, n, head_at(me, dx, dc), me)
            copy.start()
            sends.append(copy)
    for j in (1, NZ - 1):
        pl.semaphore_signal(near, inc=1, device_id={"ctx": ctx_at(y, z + j)}, device_id_type=MESH)

    flags = jnp.where(
        (kept_ref[...] == lax.broadcasted_iota(jnp.int32, (32, 32), 0))
        & (lax.broadcasted_iota(jnp.int32, (32, 32), 1) < count_ref[0]),
        1.0, 0.0,
    )
    kept = jnp.max(flags, axis=1, keepdims=True)
    bias[0] = jnp.zeros((32, QT), F32)
    bias[1] = jnp.broadcast_to((1.0 - kept) * NEG, (32, QT))
    lz[...] = jnp.zeros(lz.shape, F32)

    kcopy.wait()
    prep_keys(kraw, kx, stage)
    vcopy.wait()
    prep_values(vraw, vt, stage)

    pl.semaphore_wait(near, 2)
    for j in (2, NZ - 2):
        pl.semaphore_signal(far, inc=1, device_id={"ctx": ctx_at(y, z + j)}, device_id_type=MESH)

    def arrived(blk, hops):
        for n, (dx, dc) in enumerate(Q_HOPS):
            if dx in hops:
                q_copy(blk, n, me, head_at(me, NX - dx, dc)).wait_recv()

    swap = (3 - (x + NX - y) % NX) // 3

    def spot(blk, chip):
        r = (chip + NX - (x, y)[blk]) % NX
        b1, b0 = r // 2, r % 2
        if blk == 0:
            return 2 * b1 + (b0 + b1) % 2
        high = 1 - (b0 + b1) % 2
        return 2 * high + (1 - b1 + swap * (1 - high)) % 2

    def prepare(blk, chip):
        for c in range(2):
            prep_queries(qraw, qx, blk, chip * 2 + c, spot(blk, chip) * 2 + c)

    def y_copy(blk, h, k, at):
        dest = ctx_at(y + k, z)
        at = pl.ds(pl.multiple_of(at * GRP, GRP), GRP)
        return (
            remote(obuf.at[blk, h, at, :], r1.at[blk, k - 1, h],
                   ys_sem.at[blk, h, k - 1], yr_sem.at[blk, h, k - 1], ctx=dest),
            remote(lse.at[blk, h, :, at], l1.at[blk, k - 1, h],
                   yls_sem.at[blk, h, k - 1], ylr_sem.at[blk, h, k - 1], ctx=dest),
        )

    def y_send(blk, h, p):
        if blk == 0:
            k = (x + (0, 1, 3, 2)[p] + NY - y) % NY

            @pl.when(k > 0)
            def _():
                for copy in y_copy(0, h, k, p):
                    copy.start()
        else:
            for copy in y_copy(1, h, (2 - swap, 1 + swap, 3)[p], p):
                copy.start()

    def y_arrive(blk, h):
        for k in range(1, NY):
            for copy in y_copy(blk, h, k, 0):
                copy.wait_recv()

    def z_copy(blk, h, j):
        to = (z + j) % NZ
        at = pl.ds(pl.multiple_of(to * OWN, 16), OWN)
        dest = ctx_at(y, to)
        return (
            remote(c1.at[blk, h, at, :], r2.at[blk, j - 1, h],
                   zs_sem.at[blk, h, j - 1], zr_sem.at[blk, h, j - 1], ctx=dest),
            remote(lz.at[blk, to, h], l2.at[blk, j - 1, h],
                   zls_sem.at[blk, h, j - 1], zlr_sem.at[blk, h, j - 1], ctx=dest),
        )

    def merge_y(blk, h):
        mine = pl.ds(pl.multiple_of(spot(blk, y) * GRP, GRP), GRP)
        y_arrive(blk, h)
        combine_y(blk, h, mine, obuf, lse, r1, l1, c1, lz)
        for j in (4, 3, 5, 2, 6, 1, 7):
            for copy in z_copy(blk, h, j):
                copy.start()

    def merge_z(blk, h):
        for j in range(1, NZ):
            for copy in z_copy(blk, h, j):
                copy.wait_recv()
        combine_z(blk, h, z, c1, lz, r2, l2, out)

    tile = make_tiles(kx, vt, qx, bias, obuf, lse, s0, s1)
    own[0].wait()
    arrived(0, (0,))
    prepare(0, x)
    m = tile(score=(0, 0))
    m = tile(score=(0, 1), value=(0, 0), m=m)

    def step(i, m):
        @pl.when(i == 0)
        def _():
            arrived(0, (1, 3))
            prepare(0, (x + 3) % NX)
            prepare(0, (x + 1) % NX)

        @pl.when(i == 3)
        def _():
            arrived(0, (2,))
            prepare(0, (x + 2) % NX)

        @pl.when(i == 5)
        def _():
            own[1].wait()
            arrived(1, (0, 1, 3))
            for d in (0, 1, 3):
                prepare(1, (x + d) % NX)

        @pl.when(i == 6)
        def _():
            arrived(1, (2,))
            prepare(1, (x + 2) % NX)

        for blk, h, p, when in (
            (0, 0, 0, 1), (0, 1, 0, 2), (0, 0, 1, 2), (0, 1, 1, 3), (0, 0, 2, 4), (0, 1, 2, 5), (0, 0, 3, 5), (0, 1, 3, 6),
            (1, 0, 0, 7), (1, 1, 0, 8), (1, 0, 1, 8), (1, 1, 1, 9),
        ):
            @pl.when(i == when)
            def _():
                y_send(blk, h, p)

        m = tile(score=(i + 1, 0), value=(i, 1), m=m)
        return tile(score=(i + 1, 1), value=(i + 1, 0), m=m)

    last = 2 * TILES - 1
    m = lax.fori_loop(0, last - 1, step, m)
    y_send(1, 0, 2)
    pl.semaphore_wait(far, 2)
    merge_y(0, 0)
    merge_y(0, 1)
    m = tile(score=(last, 0), value=(last - 1, 1), m=m)
    y_send(1, 1, 2)
    m = tile(score=(last, 1), value=(last, 0), m=m)
    tile(value=(last, 1), m=m)
    merge_y(1, 0)
    merge_y(1, 1)
    for blk in range(2):
        for h in range(KV):
            merge_z(blk, h)
    for copy in sends:
        copy.wait_send()
    for blk in range(2):
        for h in range(KV):
            for k in range(1, NY):
                for copy in y_copy(blk, h, k, 0):
                    copy.wait_send()
            for j in range(1, NZ):
                for copy in z_copy(blk, h, j):
                    copy.wait_send()


def shards(q_first, q_second, k_cache, v_cache, kept_blocks, kept_count):
    anyspace = pl.BlockSpec(memory_space=pl.ANY)
    vmem = pl.BlockSpec(memory_space=pltpu.VMEM)
    dma = pltpu.SemaphoreType.DMA
    both = pl.pallas_call(
        kernel,
        out_shape=jax.ShapeDtypeStruct((2, 24, 512), BF16),
        in_specs=[anyspace] * 4 + [vmem, pl.BlockSpec(memory_space=pltpu.SMEM)],
        out_specs=vmem,
        scratch_shapes=[
            pltpu.VMEM((KEYS * KV, HD), BF16),
            pltpu.VMEM((KEYS * KV, HD), BF16),
            pltpu.VMEM((2, 8, 96, 512), BF16),
            pltpu.VMEM((KV, KEYS, 2 * HD), BF16),
            pltpu.VMEM((KV, VROWS, KEYS), BF16),
            pltpu.VMEM((1024, HD), F32),
            pltpu.VMEM((2, KV, ROWS, 2 * HD), BF16),
            pltpu.VMEM((2, 32, QT), F32),
            pltpu.VMEM((KEYS, QT), F32),
            pltpu.VMEM((KEYS, QT), F32),
            pltpu.VMEM((2, KV, ROWS, HD), BF16),
            pltpu.VMEM((2, KV, 1, ROWS), F32),
            pltpu.VMEM((2, NY - 1, KV, GRP, HD), BF16),
            pltpu.VMEM((2, NY - 1, KV, 1, GRP), F32),
            pltpu.VMEM((2, KV, GRP, HD), BF16),
            pltpu.VMEM((2, NZ, KV, 1, 128), F32),
            pltpu.VMEM((2, NZ - 1, KV, OWN, HD), BF16),
            pltpu.VMEM((2, NZ - 1, KV, 1, 128), F32),
            dma((4,)),
            dma((2, 7)), dma((2, 7)),
            dma((2, KV, 3)), dma((2, KV, 3)), dma((2, KV, 3)), dma((2, KV, 3)),
            dma((2, KV, 7)), dma((2, KV, 7)), dma((2, KV, 7)), dma((2, KV, 7)),
            pltpu.SemaphoreType.REGULAR, pltpu.SemaphoreType.REGULAR,
        ],
        compiler_params=pltpu.CompilerParams(
            collective_id=0, has_side_effects=True, vmem_limit_bytes=60 * 1024 * 1024
        ),
    )(
        q_first, q_second,
        k_cache.reshape(KEYS * KV, HD), v_cache.reshape(KEYS * KV, HD),
        kept_blocks, kept_count,
    )
    return both[0], both[1]


def solution(mesh):
    placed = (
        P("head", None),
        P("head", None),
        P("ctx", "head", None),
        P("ctx", "head", None),
        P("ctx", None),
        P("ctx"),
    )
    return jax.shard_map(
        shards,
        mesh=mesh,
        in_specs=placed,
        out_specs=(P("ctx", "head"), P("ctx", "head")),
        check_vma=False,
    )
```

time: 72.6 us -> 60.2 us (0.83)
  Pallas kernels: 68.4 us -> 57.4 us
  local copies, waits for them, and re-layouts: 2.69 us -> 1.38 us
    pallas_call x1, Pallas kernels: 68.4 us -> 57.4 us  [shards(): pl.pallas_call(kernel, out_shape=jax.ShapeDtypeStruct((2, 24, 512), BF16)...]
    unnamed x2 -> x0, local copies, waits for them, and re-layouts: 2.69 us -> none
    squeeze x0 -> x1, local copies, waits for them, and re-layouts: none -> 1.38 us  [shards(): return (both[0], both[1])]
where the time goes in v2:
time: 60.2 us; the launch traced here: 60 us
  Pallas kernels  57.4 us (95%)
  local copies, waits for them, and re-layouts  1.38 us (2%)
  between operations  1.29 us (2%)
    pallas_call x1, Pallas kernels, shards(): pl.pallas_call(kernel, out_shape=jax.ShapeDtypeStruct((2, 24, 512), BF16)...  57.4 us
    squeeze x1, local copies, waits for them, and re-layouts, shards(): return (both[0], both[1])  1.38 us

profile of v2, /device:TPU:1, one launch (start us, length us, event | category | flops | bytes accessed | tf_op | source)
XLA Modules:
  0.0 60.0 jit_solution(16982495732317465475)
XLA Ops:
  1.3 57.4 %shard_map.77 = bf16[2,24,512]{2,1,0:T(8,128)(2,1)} custom-call(bf16[96,4096]{1,0:T(8,128)(2,1)} %q0.1, bf16[96,4096]{1,0:T(8,128)(2,1)} %q1.1, bf16[8192,128]{1,0:T(8,128)(2,1)} %bitcast.6, bf16[8192,128]{1,0:T(8,128)(2,1)} %bitcast.7, s32[1,32]{1,0:T(1,128)} %kept_ref.1, s32[1]{0:T(128)S(6)} %copy.8.count_ref), custom_call_target="tpu_custom_call" | custom-call | tf_op jit(solution)/shard_map/pallas_call | solution.py:384
  58.6 1.4 %slice_bitcast_fusion = (bf16[24,512]{1,0:T(8,128)(2,1)}, bf16[24,512]{1,0:T(8,128)(2,1)}) fusion(bf16[2,24,512]{2,1,0:T(8,128)(2,1)} %shard_map.77), kind=kLoop, calls=%fused_computation | loop fusion | bytes 98304 | tf_op jit(solution)/shard_map/squeeze | solution.py:422

commit v3 on v2

--- a/solution.py
+++ b/solution.py
@@ -174,9 +174,9 @@
 
 
 def kernel(
-    q0, q1, k_hbm, v_hbm, kept_ref, count_ref, out,
+    q0, q1, k_hbm, v_hbm, kept_hbm, count_ref, out,
     kraw, vraw, qraw, kx, vt, stage, qx, bias, s0, s1, obuf, lse, r1, l1, c1, lz, r2, l2,
-    local, qs_sem, qr_sem, ys_sem, yr_sem, yls_sem, ylr_sem, zs_sem, zr_sem, zls_sem, zlr_sem, near, far,
+    local, qs_sem, qr_sem, ys_sem, yr_sem, yls_sem, ylr_sem, zs_sem, zr_sem, zls_sem, zlr_sem, near, far, kept_ref,
 ):
     me, ctx = lax.axis_index("head"), lax.axis_index("ctx")
     x, y, z = me // 2, ctx // NZ, ctx % NZ
@@ -195,7 +195,9 @@
     cols = pl.ds(pl.multiple_of(me * 512, 512), 512)
     for blk, q in enumerate((q0, q1)):
         own.append(pltpu.make_async_copy(q.at[:, cols], qraw.at[blk, me], local.at[2 + blk]))
+    kept_copy = pltpu.make_async_copy(kept_hbm, kept_ref, local.at[4])
     own[0].start()
+    kept_copy.start()
     kcopy.start()
     vcopy.start()
     own[1].start()
@@ -218,6 +220,7 @@
     for j in (1, NZ - 1):
         pl.semaphore_signal(near, inc=1, device_id={"ctx": ctx_at(y, z + j)}, device_id_type=MESH)
 
+    kept_copy.wait()
     flags = jnp.where(
         (kept_ref[...] == lax.broadcasted_iota(jnp.int32, (32, 32), 0))
         & (lax.broadcasted_iota(jnp.int32, (32, 32), 1) < count_ref[0]),
@@ -315,37 +318,45 @@
     m = tile(score=(0, 0))
     m = tile(score=(0, 1), value=(0, 0), m=m)
 
-    def step(i, m):
-        @pl.when(i == 0)
-        def _():
+    due = {
+        1: ((0, 0, 0),),
+        2: ((0, 1, 0), (0, 0, 1)),
+        3: ((0, 1, 1),),
+        4: ((0, 0, 2),),
+        5: ((0, 1, 2), (0, 0, 3)),
+        6: ((0, 1, 3),),
+        7: ((1, 0, 0),),
+        8: ((1, 1, 0), (1, 0, 1)),
+        9: ((1, 1, 1),),
+    }
+
+    def between(at):
+        for blk, h, p in due.get(at, ()):
+            y_send(blk, h, p)
+        if at == 0:
+            own[1].wait()
+            arrived(1, (0,))
+            prepare(1, x)
             arrived(0, (1, 3))
+            prepare(0, (x + 1) % NX)
             prepare(0, (x + 3) % NX)
-            prepare(0, (x + 1) % NX)
-
-        @pl.when(i == 3)
-        def _():
+        if at == 3:
             arrived(0, (2,))
             prepare(0, (x + 2) % NX)
-
-        @pl.when(i == 5)
-        def _():
-            own[1].wait()
-            arrived(1, (0, 1, 3))
-            for d in (0, 1, 3):
-                prepare(1, (x + d) % NX)
-
-        @pl.when(i == 6)
-        def _():
+        if at == 5:
+            arrived(1, (1, 3))
+            prepare(1, (x + 1) % NX)
+            prepare(1, (x + 3) % NX)
+        if at == 6:
             arrived(1, (2,))
             prepare(1, (x + 2) % NX)
 
-        for blk, h, p, when in (
-            (0, 0, 0, 1), (0, 1, 0, 2), (0, 0, 1, 2), (0, 1, 1, 3), (0, 0, 2, 4), (0, 1, 2, 5), (0, 0, 3, 5), (0, 1, 3, 6),
-            (1, 0, 0, 7), (1, 1, 0, 8), (1, 0, 1, 8), (1, 1, 1, 9),
-        ):
-            @pl.when(i == when)
+    def step(i, m):
+        for at in range(10):
+
+            @pl.when(i == at)
             def _():
-                y_send(blk, h, p)
+                between(at)
 
         m = tile(score=(i + 1, 0), value=(i, 1), m=m)
         return tile(score=(i + 1, 1), value=(i + 1, 0), m=m)
@@ -353,11 +364,11 @@
     last = 2 * TILES - 1
     m = lax.fori_loop(0, last - 1, step, m)
     y_send(1, 0, 2)
+    m = tile(score=(last, 0), value=(last - 1, 1), m=m)
+    y_send(1, 1, 2)
     pl.semaphore_wait(far, 2)
     merge_y(0, 0)
     merge_y(0, 1)
-    m = tile(score=(last, 0), value=(last - 1, 1), m=m)
-    y_send(1, 1, 2)
     m = tile(score=(last, 1), value=(last, 0), m=m)
     tile(value=(last, 1), m=m)
     merge_y(1, 0)
@@ -384,7 +395,7 @@
     both = pl.pallas_call(
         kernel,
         out_shape=jax.ShapeDtypeStruct((2, 24, 512), BF16),
-        in_specs=[anyspace] * 4 + [vmem, pl.BlockSpec(memory_space=pltpu.SMEM)],
+        in_specs=[anyspace] * 5 + [pl.BlockSpec(memory_space=pltpu.SMEM)],
         out_specs=vmem,
         scratch_shapes=[
             pltpu.VMEM((KEYS * KV, HD), BF16),
@@ -405,11 +416,12 @@
             pltpu.VMEM((2, NZ, KV, 1, 128), F32),
             pltpu.VMEM((2, NZ - 1, KV, OWN, HD), BF16),
             pltpu.VMEM((2, NZ - 1, KV, 1, 128), F32),
-            dma((4,)),
+            dma((5,)),
             dma((2, 7)), dma((2, 7)),
             dma((2, KV, 3)), dma((2, KV, 3)), dma((2, KV, 3)), dma((2, KV, 3)),
             dma((2, KV, 7)), dma((2, KV, 7)), dma((2, KV, 7)), dma((2, KV, 7)),
             pltpu.SemaphoreType.REGULAR, pltpu.SemaphoreType.REGULAR,
+            pltpu.VMEM((1, 32), jnp.int32),
         ],
         compiler_params=pltpu.CompilerParams(
             collective_id=0, has_side_effects=True, vmem_limit_bytes=60 * 1024 * 1024

time: 60.2 us -> 59.3 us (0.985)
  Pallas kernels: 57.4 us -> 56.5 us
    pallas_call x1, Pallas kernels: 57.4 us -> 56.5 us  [shards(): pl.pallas_call(kernel, out_shape=jax.ShapeDtypeStruct((2, 24, 512), BF16)...]
where the time goes in v3:
time: 59.3 us; the launch traced here: 59.1 us
  Pallas kernels  56.5 us (95%)
  local copies, waits for them, and re-layouts  1.38 us (2%)
  between operations  1.29 us (2%)
    pallas_call x1, Pallas kernels, shards(): pl.pallas_call(kernel, out_shape=jax.ShapeDtypeStruct((2, 24, 512), BF16)...  56.5 us
    squeeze x1, local copies, waits for them, and re-layouts, shards(): return (both[0], both[1])  1.38 us

profile of v3, /device:TPU:1, one launch (start us, length us, event | category | flops | bytes accessed | tf_op | source)
XLA Modules:
  0.0 59.1 jit_solution(8517314101692133790)
XLA Ops:
  1.3 56.5 %shard_map.77 = bf16[2,24,512]{2,1,0:T(8,128)(2,1)} custom-call(bf16[96,4096]{1,0:T(8,128)(2,1)} %q0.1, bf16[96,4096]{1,0:T(8,128)(2,1)} %q1.1, bf16[8192,128]{1,0:T(8,128)(2,1)} %bitcast.6, bf16[8192,128]{1,0:T(8,128)(2,1)} %bitcast.7, s32[1,32]{1,0:T(1,128)} %kept_hbm.1, s32[1]{0:T(128)S(6)} %copy.8.count_ref), custom_call_target="tpu_custom_call" | custom-call | tf_op jit(solution)/shard_map/pallas_call | solution.py:395
  57.7 1.4 %slice_bitcast_fusion = (bf16[24,512]{1,0:T(8,128)(2,1)}, bf16[24,512]{1,0:T(8,128)(2,1)}) fusion(bf16[2,24,512]{2,1,0:T(8,128)(2,1)} %shard_map.77), kind=kLoop, calls=%fused_computation | loop fusion | bytes 98304 | tf_op jit(solution)/shard_map/squeeze | solution.py:434

commit v4 on v3

--- a/solution.py
+++ b/solution.py
@@ -278,13 +278,35 @@
                 for copy in y_copy(0, h, k, p):
                     copy.start()
         else:
-            for copy in y_copy(1, h, (2 - swap, 1 + swap, 3)[p], p):
+            for copy in y_copy(1, h, (2 - swap, 1 + swap)[p], p):
                 copy.start()
 
+    def y_tail(h, part):
+        off, n = ((0, QT), (QT, GRP - QT))[part]
+        dest = ctx_at(y + 3, z)
+        made = [remote(obuf.at[1, h, pl.ds(2 * GRP + off, n), :], r1.at[1, 2, h, pl.ds(off, n), :],
+                       ys_sem.at[1, h, 2 + part], yr_sem.at[1, h, 2 + part], ctx=dest)]
+        if part:
+            made.append(remote(lse.at[1, h, :, pl.ds(2 * GRP, GRP)], l1.at[1, 2, h],
+                               yls_sem.at[1, h, 2], ylr_sem.at[1, h, 2], ctx=dest))
+        return made
+
+    def y_tail_send(h, part):
+        for copy in y_tail(h, part):
+            copy.start()
+
+    def y_all(blk, h):
+        copies = []
+        for k in range(1, NY):
+            if blk == 1 and k == 3:
+                copies += y_tail(h, 0) + y_tail(h, 1)
+            else:
+                copies += y_copy(blk, h, k, 0)
+        return copies
+
     def y_arrive(blk, h):
-        for k in range(1, NY):
-            for copy in y_copy(blk, h, k, 0):
-                copy.wait_recv()
+        for copy in y_all(blk, h):
+            copy.wait_recv()
 
     def z_copy(blk, h, j):
         to = (z + j) % NZ
@@ -350,6 +372,8 @@
         if at == 6:
             arrived(1, (2,))
             prepare(1, (x + 2) % NX)
+        if at == 9:
+            y_tail_send(0, 0)
 
     def step(i, m):
         for at in range(10):
@@ -363,9 +387,10 @@
 
     last = 2 * TILES - 1
     m = lax.fori_loop(0, last - 1, step, m)
-    y_send(1, 0, 2)
+    y_tail_send(0, 1)
+    y_tail_send(1, 0)
     m = tile(score=(last, 0), value=(last - 1, 1), m=m)
-    y_send(1, 1, 2)
+    y_tail_send(1, 1)
     pl.semaphore_wait(far, 2)
     merge_y(0, 0)
     merge_y(0, 1)
@@ -380,9 +405,8 @@
         copy.wait_send()
     for blk in range(2):
         for h in range(KV):
-            for k in range(1, NY):
-                for copy in y_copy(blk, h, k, 0):
-                    copy.wait_send()
+            for copy in y_all(blk, h):
+                copy.wait_send()
             for j in range(1, NZ):
                 for copy in z_copy(blk, h, j):
                     copy.wait_send()
@@ -418,7 +442,7 @@
             pltpu.VMEM((2, NZ - 1, KV, 1, 128), F32),
             dma((5,)),
             dma((2, 7)), dma((2, 7)),
-            dma((2, KV, 3)), dma((2, KV, 3)), dma((2, KV, 3)), dma((2, KV, 3)),
+            dma((2, KV, 4)), dma((2, KV, 4)), dma((2, KV, 3)), dma((2, KV, 3)),
             dma((2, KV, 7)), dma((2, KV, 7)), dma((2, KV, 7)), dma((2, KV, 7)),
             pltpu.SemaphoreType.REGULAR, pltpu.SemaphoreType.REGULAR,
             pltpu.VMEM((1, 32), jnp.int32),

time: 59.3 us -> 59.4 us (level)
  no operation moved by 1% of the time
where the time goes in v4:
time: 59.4 us; the launch traced here: 59.2 us
  Pallas kernels  56.6 us (95%)
  local copies, waits for them, and re-layouts  1.38 us (2%)
  between operations  1.29 us (2%)
    pallas_call x1, Pallas kernels, shards(): pl.pallas_call(kernel, out_shape=jax.ShapeDtypeStruct((2, 24, 512), BF16)...  56.6 us
    squeeze x1, local copies, waits for them, and re-layouts, shards(): return (both[0], both[1])  1.38 us

profile of v4, /device:TPU:1, one launch (start us, length us, event | category | flops | bytes accessed | tf_op | source)
XLA Modules:
  0.0 59.2 jit_solution(15868055706770847115)
XLA Ops:
  1.3 56.6 %shard_map.77 = bf16[2,24,512]{2,1,0:T(8,128)(2,1)} custom-call(bf16[96,4096]{1,0:T(8,128)(2,1)} %q0.1, bf16[96,4096]{1,0:T(8,128)(2,1)} %q1.1, bf16[8192,128]{1,0:T(8,128)(2,1)} %bitcast.6, bf16[8192,128]{1,0:T(8,128)(2,1)} %bitcast.7, s32[1,32]{1,0:T(1,128)} %kept_hbm.1, s32[1]{0:T(128)S(6)} %copy.8.count_ref), custom_call_target="tpu_custom_call" | custom-call | tf_op jit(solution)/shard_map/pallas_call | solution.py:419
  57.8 1.4 %slice_bitcast_fusion = (bf16[24,512]{1,0:T(8,128)(2,1)}, bf16[24,512]{1,0:T(8,128)(2,1)}) fusion(bf16[2,24,512]{2,1,0:T(8,128)(2,1)} %shard_map.77), kind=kLoop, calls=%fused_computation | loop fusion | bytes 98304 | tf_op jit(solution)/shard_map/squeeze | solution.py:458
